TPU v7x, 32 devices: a whole 2x2x4 slice. The times are simulated.
32 devices in a mesh: ctx: 4 (over y, core), exp: 8 (over z, x).
Axes of the slice: x: 2, y: 2, z: 4, core: 2. Of those that a mesh axis runs over, the one named last changes fastest.
Arguments:
- queries: bfloat16 [512, 64, 576], P('ctx', 'exp'), may hold values from -1024 to 1024
- latents: bfloat16 [512, 576], P('ctx'), may hold values from -6.1 to 6.1
- block_starts: int32 [8], replicated, may hold values from 0 to 448, as said below
- w_uv: bfloat16 [64, 512, 128], P('exp'), may hold values from -0.25 to 0.25
- moe_tokens: bfloat16 [1024, 7168], P('exp'), may hold values from -6 to 6
- expert_ids: int32 [1024, 2], P('exp'), may hold values from 0 to 7, as said below
- gate_weights: float32 [1024, 2], P('exp'), may hold values from 0.2 to 1
- w_gate: bfloat16 [8, 7168, 512], P('exp', None, 'ctx'), may hold values from -0.0625 to 0.0625
- w_up: bfloat16 [8, 7168, 512], P('exp', None, 'ctx'), may hold values from -0.0625 to 0.0625
- w_down: bfloat16 [8, 512, 7168], P('exp', 'ctx'), may hold values from -0.25 to 0.25
Outputs:
- attended: bfloat16 [512, 64, 128], P('ctx', 'exp')
- moe_out: bfloat16 [1024, 7168], P('exp', 'ctx')
Inputs may be any that keep to these rules, and one draw needn't show every extreme that they name: Token t has position block_starts[t // 64] + t % 64; block_starts is a permutation of the multiples of 64 below 512. `expert_ids`: each row names 2 different experts. In the rows of one index of exp, one expert, the same for every index, is named by exactly 48 rows, no expert by more, and the other experts' counts differ by at most one.
All inputs are finite; a program needn't handle non-finite values.
Results may differ from a plain program's by a relative error of at most 0.018.
Values may be sent and summed in bfloat16 or wider, within the bound.
A program may use at most 128 MiB of HBM per device.

v0:
```python
import math

import jax
import jax.numpy as jnp
from jax import lax
from jax.sharding import PartitionSpec as P

score_scale = (0.1 * math.log(40.0) + 1.0) ** 2 / math.sqrt(192.0)
neg_fill = -1e30


def token_positions(block_starts, token_index, half_block):
    block_index = token_index // half_block
    matches = block_index[:, None] == jnp.arange(block_starts.shape[0], dtype=jnp.int32)[None, :]
    first_pos = jnp.sum(jnp.where(matches, block_starts[None, :], 0), axis=1)
    return first_pos + token_index % half_block


def slot_targets(expert_ids, expert_count, capacity):
    token_count, picks = expert_ids.shape
    flat_ids = expert_ids.reshape(token_count * picks)
    onehot = (flat_ids[:, None] == jnp.arange(expert_count, dtype=jnp.int32)[None, :]).astype(
        jnp.int32
    )
    earlier = jnp.cumsum(onehot, axis=0) - onehot
    slot_index = jnp.sum(earlier * onehot, axis=1)
    return flat_ids * capacity + slot_index


def shards(
    queries, latents, block_starts, w_uv, moe_tokens, expert_ids, gate_weights, w_gate, w_up, w_down
):
    query_tokens, head_count, entry_width = queries.shape
    lat_width = w_uv.shape[1]
    half_block = query_tokens // 2
    row_total = query_tokens * head_count
    flat_queries = queries.reshape(row_total, entry_width)
    own_index = lax.axis_index("ctx") * query_tokens + jnp.arange(query_tokens, dtype=jnp.int32)
    own_positions = token_positions(block_starts, own_index, half_block)
    query_positions = jnp.repeat(own_positions, head_count)
    shard_piece = lax.all_gather(latents, "ctx", axis=0, tiled=True)
    key_positions = token_positions(
        block_starts, jnp.arange(shard_piece.shape[0], dtype=jnp.int32), half_block
    )
    top_score = jnp.full((row_total,), neg_fill, jnp.float32)
    scores = (
        lax.dot_general(
            flat_queries, shard_piece, (((1,), (1,)), ((), ())), preferred_element_type=jnp.float32
        )
        * score_scale
    )
    visible = key_positions[None, :] <= query_positions[:, None]
    masked = jnp.where(visible, scores, neg_fill)
    new_top = jnp.maximum(top_score, jnp.max(masked, axis=1))
    weights = jnp.where(visible, jnp.exp(masked - new_top[:, None]), 0.0)
    totals = jnp.sum(weights, axis=1)
    blended = jnp.dot(
        weights.astype(jnp.bfloat16), shard_piece[:, :lat_width], preferred_element_type=jnp.float32
    )
    top_score, totals, blended = (new_top, totals, blended)
    latent_out = (
        (blended / totals[:, None])
        .astype(jnp.bfloat16)
        .reshape(query_tokens, head_count, lat_width)
    )
    attended = jnp.einsum(
        "shl,hlv->shv", latent_out, w_uv, preferred_element_type=jnp.float32
    ).astype(jnp.bfloat16)
    token_count, picks = expert_ids.shape
    model_width = moe_tokens.shape[1]
    expert_count = lax.axis_size("exp")
    capacity = 3 * token_count * picks // (2 * expert_count)
    targets = slot_targets(expert_ids, expert_count, capacity)
    source_row = jnp.arange(token_count * picks, dtype=jnp.int32) // picks
    filled = jnp.zeros((expert_count * capacity,), jnp.int32).at[targets].set(source_row + 1)
    occupied = filled > 0
    gate_matrix = w_gate[0]
    up_matrix = w_up[0]
    down_matrix = w_down[0]
    picked_rows = moe_tokens[jnp.where(occupied, filled - 1, 0)]
    outgoing = jnp.where(occupied[:, None], picked_rows, 0).reshape(
        expert_count, capacity, model_width
    )
    arrived = lax.all_to_all(outgoing, "exp", split_axis=0, concat_axis=0, tiled=True)
    senders, slot_count, width_in = arrived.shape
    flat_rows = arrived.reshape(senders * slot_count, width_in)
    gate_h = jnp.dot(flat_rows, gate_matrix, preferred_element_type=jnp.float32)
    up_h = jnp.dot(flat_rows, up_matrix, preferred_element_type=jnp.float32)
    hidden = (jax.nn.silu(gate_h) * up_h).astype(jnp.bfloat16)
    rounded = jnp.dot(hidden, down_matrix, preferred_element_type=jnp.float32).astype(jnp.bfloat16)
    rounded = lax.optimization_barrier(rounded.reshape(senders, slot_count, width_in))
    summed = lax.psum_scatter(
        rounded.astype(jnp.float32).astype(jnp.bfloat16), "ctx", scatter_dimension=2, tiled=True
    ).astype(jnp.float32)
    returned = lax.all_to_all(
        summed.astype(jnp.bfloat16), "exp", split_axis=0, concat_axis=0, tiled=True
    ).astype(summed.dtype)
    out_width = returned.shape[2]
    gathered = returned.reshape(expert_count * capacity, out_width)[targets].reshape(
        token_count, picks, out_width
    )
    weighted = jnp.sum(gathered * gate_weights[:, :, None], axis=1)
    return (attended, weighted.astype(jnp.bfloat16))


def solution(mesh):
    in_specs = (
        P("ctx", "exp", None),
        P("ctx", None),
        P(),
        P("exp", None, None),
        P("exp", None),
        P("exp", None),
        P("exp", None),
        P("exp", None, "ctx"),
        P("exp", None, "ctx"),
        P("exp", "ctx", None),
    )
    out_specs = (P("ctx", "exp", None), P("exp", "ctx"))
    return jax.shard_map(shards, mesh=mesh, in_specs=in_specs, out_specs=out_specs, check_vma=False)
```

profile of v0, /device:TPU:0, one launch (start us, length us, event | category | flops | bytes accessed | tf_op | source)
XLA Modules:
  0.0 277.9 jit_solution(2262390735717039170)
XLA Ops:
  7.2 0.9 copy.25
  8.1 0.1 eq.65
  8.3 0.1 eq.61
  8.4 0.7 broadcast_multiply_fusion
  9.1 0.6 reduce-window.6
  9.7 0.2 slice_reduce_fusion
  10.1 0.1 mul.48
  10.3 1.4 scatter_custom_fusion
  11.9 6.5 %gather_fusion = bf16[384,7168]{1,0:T(8,128)(2,1)} fusion(bf16[128,7168]{1,0:T(8,128)(2,1)S(1)} %copy-done, s32[1024]{0:T(1024)S(1)} %pad_clamp_fusion.1), kind=kCustom, calls=%fused_computation | custom fusion | bytes 11011584 | tf_op jit(solution)/shard_map/gather | solution.py:80
  18.3 3.0 %broadcast_select_fusion = bf16[8,48,7168]{2,1,0:T(8,128)(2,1)S(1)} fusion(bf16[8,48,7168]{2,1,0:T(8,128)(2,1)} %bitcast.46, pred[8,48]{1,0:T(8,128)(4,1)S(1)} %broadcast_in_dim.78), kind=kLoop, calls=%fused_computation.4 | loop fusion | flops 2752512 | bytes 11010432 | tf_op jit(solution)/shard_map/jit(_where)/select_n | solution.py:81
  21.3 128.5 %all_to_all.10 = bf16[8,48,7168]{2,1,0:T(8,128)(2,1)S(1)} all-to-all(bf16[8,48,7168]{2,1,0:T(8,128)(2,1)S(1)} %broadcast_select_fusion), channel_id=1, replica_groups=mesh['ctx'=4,'exp'=8] {'exp'}, dimensions={0} | all-to-all | bytes 11010048 | tf_op jit(solution)/shard_map/all_to_all | solution.py:84
  149.8 2.5 copy-done.1
  152.3 1.6 fusion.3
  153.8 11.9 %convolution_convert_fusion = bf16[384,7168]{1,0:T(8,128)(2,1)} fusion(bf16[1,128,7168]{2,1,0:T(8,128)(2,1)} %param.19, bf16[384,7168]{1,0:T(8,128)(2,1)} %bitcast.45, bf16[1,7168,128]{2,1,0:T(8,128)(2,1)} %param.18, f32[384,128]{1,0:T(8,128)S(1)} %fusion.3), kind=kOutput, calls=%fused_computation.3 | convolution fusion | flops 1412333568 | bytes 14876672 | tf_op jit(solution)/shard_map/dot_general | solution.py:90
  165.8 0.6 copy-done.6
  166.7 0.4 copy-done.3
  167.0 2.0 copy.22
  169.0 48.8 %reduce-scatter.2.cloned.1.call-done = bf16[8,48,1792]{2,1,0:T(8,128)(2,1)} async-done(((bf16[8,48,7168]{2,1,0:T(8,128)(2,1)}), bf16[8,48,1792]{2,1,0:T(8,128)(2,1)}) %reduce-scatter.2.cloned.1.call-update) | async-done | bytes 1376272 | tf_op jit(solution)/shard_map/reduce_scatter | solution.py:92
  217.8 5.5 %all-to-all-start.1 = ((bf16[8,48,1792]{2,1,0:T(8,128)(2,1)}), bf16[8,48,1792]{2,1,0:T(8,128)(2,1)S(1)}, u32[]{:S(2)}, u32[]{:S(2)}) async-start(bf16[8,48,1792]{2,1,0:T(8,128)(2,1)} %reduce-scatter.2.cloned.1.call-done), calls=%async_computation.2 | async-start | bytes 2752512 | tf_op jit(solution)/shard_map/all_to_all | solution.py:95
  223.4 6.9 %all_gather.3 = bf16[512,576]{0,1:T(8,128)(2,1)S(1)} all-gather(bf16[128,576]{0,1:T(8,128)(2,1)S(1)} %copy-done.4), channel_id=1, replica_groups=mesh['ctx'=4,'exp'=8] {'ctx'}, dimensions={0}, use_global_device_ids=true | all-gather | bytes 737280 | tf_op jit(solution)/shard_map/all_gather | solution.py:41
  230.3 2.4 fusion.5
  232.7 0.6 fusion.9
  233.4 0.9 fusion.6
  234.3 0.3 copy-done.7
  234.6 0.7 fusion.11
  235.3 0.9 copy.28
  236.2 0.1 copy.27
  236.3 19.6 %all-to-all-done.1 = bf16[8,48,1792]{2,1,0:T(8,128)(2,1)S(1)} async-done(((bf16[8,48,1792]{2,1,0:T(8,128)(2,1)}), bf16[8,48,1792]{2,1,0:T(8,128)(2,1)S(1)}, u32[]{:S(2)}, u32[]{:S(2)}) %all-to-all-start.1) | async-done | bytes 1376288 | tf_op jit(solution)/shard_map/all_to_all | solution.py:95
  256.0 1.8 bitcast_convert_fusion
  257.8 5.1 %gather_fusion.1 = f32[256,1792]{1,0:T(8,128)} fusion(f32[384,1792]{1,0:T(8,128)} %bitcast_convert_fusion, s32[1024]{0:T(1024)S(1)} %pad_clamp_fusion), kind=kCustom, calls=%fused_computation.1 | custom fusion | bytes 3671040 | tf_op jit(solution)/shard_map/gather | solution.py:99
  262.9 3.3 %reshape.137 = f32[128,2,1792]{2,1,0:T(2,128)} reshape(f32[256,1792]{1,0:T(8,128)} %gather_fusion.1) | data formatting | bytes 3670016 | tf_op jit(solution)/shard_map/reshape | solution.py:99
  266.2 4.9 %multiply_reduce_fusion = bf16[128,1792]{1,0:T(8,128)(2,1)} fusion(f32[128,2,1792]{2,1,0:T(2,128)} %reshape.137, f32[128,2]{1,0:T(8,128)S(1)} %copy.27), kind=kLoop, calls=%fused_computation.13 | loop fusion | flops 688128 | bytes 2294784 | tf_op jit(solution)/shard_map/reduce_sum | solution.py:102
  (35 shorter events, 0.8 us)
Async XLA Ops:
  7.2 4.7 %copy-start = (bf16[128,7168]{1,0:T(8,128)(2,1)S(1)}, bf16[128,7168]{1,0:T(8,128)(2,1)}, u32[]{:S(2)}) copy-start(bf16[128,7168]{1,0:T(8,128)(2,1)} %param.14) | copy-start | bytes 5505028
  7.2 210.7 %reduce-scatter.2.cloned.1.call-start = ((), (), s32[]{:S(2)}) async-start(), calls=%async_computation.3 | async-start | bytes 6881280 | tf_op jit(solution)/shard_map/reduce_scatter | solution.py:92
  21.3 130.9 %copy-start.2 = (bf16[1,7168,128]{2,1,0:T(8,128)(2,1)S(1)}, bf16[1,7168,128]{2,1,0:T(8,128)(2,1)}, u32[]{:S(2)}) copy-start(bf16[1,7168,128]{2,1,0:T(8,128)(2,1)} %param.17) | copy-start | bytes 5505028
  149.8 2.5 copy-start.1
  165.7 0.7 copy-start.6
  165.7 1.3 copy-start.3
  167.0 56.4 %copy-start.4 = (bf16[128,576]{0,1:T(8,128)(2,1)S(1)}, bf16[128,576]{0,1:T(8,128)(2,1)}, u32[]{:S(2)}) copy-start(bf16[128,576]{0,1:T(8,128)(2,1)} %param.11) | copy-start | bytes 442372
  217.8 38.1 %all-to-all-start.1 = ((bf16[8,48,1792]{2,1,0:T(8,128)(2,1)}), bf16[8,48,1792]{2,1,0:T(8,128)(2,1)S(1)}, u32[]{:S(2)}, u32[]{:S(2)}) async-start(bf16[8,48,1792]{2,1,0:T(8,128)(2,1)} %reduce-scatter.2.cloned.1.call-done), calls=%async_computation.2 | async-start | bytes 2752512 | tf_op jit(solution)/shard_map/all_to_all | solution.py:95
  233.4 1.2 copy-start.7
  234.6 1.6 copy-start.5
Sparse Core Ops, SparseCore 0:
  165.9 51.9 reduce-scatter.1
where the time goes:
time: 278 us
  blocking collectives  135 us (49%)
  waiting for transfers between devices  68.5 us (25%)
  local copies, waits for them, and re-layouts  24.9 us (9%)
  matrix products  17.5 us (6%)
  between operations  14.2 us (5%)
  other arithmetic  12 us (4%)
  starting transfers between devices  5.54 us (2%)
    all_to_all x1, blocking collectives, shards(): lax.all_to_all(outgoing, 'exp', split_axis=0, concat_axis=0, tiled=True)  128 us
    reduce_scatter x1, waiting for transfers between devices, shards(): lax.psum_scatter(rounded.astype(jnp.float32).astype(jnp.bfloat16), 'ctx',...  48.8 us
    all_to_all x1, waiting for transfers between devices, shards(): lax.all_to_all(summed.astype(jnp.bfloat16), 'exp', split_axis=0, concat_a...  19.6 us
    dot_general x1, matrix products, shards(): jnp.dot(hidden, down_matrix, preferred_element_type=jnp.float32)  11.9 us
    unnamed x20, local copies, waits for them, and re-layouts  7.62 us
    all_gather x1, blocking collectives, shards(): shard_piece = lax.all_gather(latents, 'ctx', axis=0, tiled=True)  6.91 us
    gather x1, local copies, waits for them, and re-layouts, shards(): picked_rows = moe_tokens[jnp.where(occupied, filled - 1, 0)]  6.47 us
  transfers between devices with their start and end apart: 2, of which 2 were waited for; matrix products, arithmetic and copies ran while one was open for 3% of the time, Pallas kernels for 0%

commit v1 on v0

--- a/solution.py
+++ b/solution.py
@@ -1,8 +1,11 @@
+import functools
 import math
 
 import jax
 import jax.numpy as jnp
 from jax import lax
+from jax.experimental import pallas as pl
+from jax.experimental.pallas import tpu as pltpu
 from jax.sharding import PartitionSpec as P
 
 score_scale = (0.1 * math.log(40.0) + 1.0) ** 2 / math.sqrt(192.0)
@@ -27,9 +30,7 @@
     return flat_ids * capacity + slot_index
 
 
-def shards(
-    queries, latents, block_starts, w_uv, moe_tokens, expert_ids, gate_weights, w_gate, w_up, w_down
-):
+def attention(queries, latents, block_starts, w_uv):
     query_tokens, head_count, entry_width = queries.shape
     lat_width = w_uv.shape[1]
     half_block = query_tokens // 2
@@ -66,6 +67,10 @@
     attended = jnp.einsum(
         "shl,hlv->shv", latent_out, w_uv, preferred_element_type=jnp.float32
     ).astype(jnp.bfloat16)
+    return attended
+
+
+def routed_plain(moe_tokens, expert_ids, gate_weights, w_gate, w_up, w_down):
     token_count, picks = expert_ids.shape
     model_width = moe_tokens.shape[1]
     expert_count = lax.axis_size("exp")
@@ -100,7 +105,256 @@
         token_count, picks, out_width
     )
     weighted = jnp.sum(gathered * gate_weights[:, :, None], axis=1)
-    return (attended, weighted.astype(jnp.bfloat16))
+    return weighted.astype(jnp.bfloat16)
+
+
+def flip_bits(index, bits):
+    flipped = index
+    for bit in range(bits.bit_length()):
+        if (bits >> bit) % 2:
+            flipped = flipped + (1 << bit) * (1 - 2 * ((index // (1 << bit)) % 2))
+    return flipped
+
+
+def step_order(count):
+    half = count // 2
+    near, far = list(range(1, half)), list(range(half, count))
+    order = []
+    for at in range(half):
+        if at < len(near):
+            order.append(near[at])
+        order.append(far[at])
+    return order
+
+
+def dot_f32(left, right):
+    return jnp.dot(left, right, preferred_element_type=jnp.float32)
+
+
+def routed_kernel(
+    count, outgoing, own_rows, combine, gate_hbm, up_hbm, down_hbm, out_ref,
+    gate_w, up_w, down_w, arrived, kept, core_send, core_recv, row_send, row_recv,
+    back_send, returned, load_sem, own_sem,
+    out_s, out_r, side_s, side_r, near_s, near_r, relay_s, relay_r,
+    core_s, core_r, row_s, row_r, back_s, back_r,
+):
+    me = lax.axis_index("exp")
+    ctx = lax.axis_index("ctx")
+    core = ctx % 2
+    other_core = ctx + 1 - 2 * core
+    other_row = (ctx + 2) % 4
+    width = outgoing.shape[2]
+
+    loads = [
+        pltpu.make_async_copy(gate_hbm.at[0], gate_w, load_sem.at[0]),
+        pltpu.make_async_copy(up_hbm.at[0], up_w, load_sem.at[1]),
+        pltpu.make_async_copy(down_hbm.at[0], down_w, load_sem.at[2]),
+    ]
+    for load in loads:
+        load.start()
+
+    barrier = pltpu.get_barrier_semaphore()
+    for k in range(1, count):
+        pl.semaphore_signal(
+            barrier, inc=1, device_id={"exp": flip_bits(me, k), "ctx": ctx},
+            device_id_type=pl.DeviceIdType.MESH,
+        )
+    for peer in (other_core, other_row):
+        pl.semaphore_signal(
+            barrier, inc=1, device_id={"exp": me, "ctx": peer},
+            device_id_type=pl.DeviceIdType.MESH,
+        )
+    pl.semaphore_wait(barrier, count + 1)
+
+    def remote(source, target, send, recv, exp, ctx_at):
+        return pltpu.make_async_remote_copy(
+            src_ref=source, dst_ref=target, send_sem=send, recv_sem=recv,
+            device_id={"exp": exp, "ctx": ctx_at}, device_id_type=pl.DeviceIdType.MESH,
+        )
+
+    def dispatch(k):
+        to = flip_bits(me, k)
+        return remote(
+            outgoing.at[to], arrived.at[ctx, me], out_s.at[k], out_r.at[k], to, ctx
+        )
+
+    def across(k):
+        block = arrived.at[ctx, flip_bits(me, k)]
+        return remote(block, block, side_s.at[k], side_r.at[k], me, other_row)
+
+    def beside(k):
+        block = arrived.at[ctx, flip_bits(me, k)]
+        return remote(block, block, near_s.at[k], near_r.at[k], me, other_core)
+
+    def relay(k):
+        block = arrived.at[other_row, flip_bits(me, k)]
+        return remote(block, block, relay_s.at[k], relay_r.at[k], me, other_core)
+
+    def core_swap(k):
+        return remote(
+            core_send.at[k], core_recv.at[k], core_s.at[k], core_r.at[k], me, other_core
+        )
+
+    def row_swap(k):
+        return remote(
+            row_send.at[k], row_recv.at[k], row_s.at[k], row_r.at[k], me, other_row
+        )
+
+    def give_back(k):
+        to = flip_bits(me, k)
+        return remote(
+            back_send.at[k], returned.at[me], back_s.at[k], back_r.at[k], to, ctx
+        )
+
+    order = step_order(count)
+    for k in order:
+        dispatch(k).start()
+
+    def columns(at):
+        return pl.ds(pl.multiple_of(at * width, 128), width)
+
+    def experts(k):
+        at = flip_bits(me, k)
+        rows = outgoing.shape[1]
+        gate_h = jnp.zeros((rows, gate_w.shape[1]), jnp.float32)
+        up_h = jnp.zeros((rows, up_w.shape[1]), jnp.float32)
+        for quarter in range(4):
+            span = pl.ds(quarter * width, width)
+            block = own_rows[:, span] if k == 0 else arrived[quarter, at]
+            gate_h += dot_f32(block, gate_w[span, :])
+            up_h += dot_f32(block, up_w[span, :])
+        hidden = (gate_h / (1.0 + jnp.exp(-gate_h)) * up_h).astype(jnp.bfloat16)
+        mate = 1 - core
+        for side in range(2):
+            core_send[k, side] = dot_f32(hidden, down_w[:, columns(mate + 2 * side)]).astype(
+                jnp.bfloat16
+            )
+        core_swap(k).start()
+        for side in range(2):
+            kept[k, side] = dot_f32(hidden, down_w[:, columns(core + 2 * side)]).astype(
+                jnp.bfloat16
+            )
+
+    def pair_sum(k, side):
+        return kept[k, side].astype(jnp.float32) + core_recv[k, side].astype(jnp.float32)
+
+    def forward(k):
+        if k:
+            dispatch(k).wait_recv()
+            across(k).start()
+            beside(k).start()
+
+    def pass_on(k):
+        if k:
+            across(k).wait_recv()
+            relay(k).start()
+
+    def compute(k):
+        if k:
+            beside(k).wait_recv()
+            relay(k).wait_recv()
+        experts(k)
+
+    def sum_cores(k):
+        core_swap(k).wait_recv()
+        row_send[k] = pair_sum(k, 1 - ctx // 2).astype(jnp.bfloat16)
+        row_swap(k).start()
+
+    def sum_rows(k):
+        row_swap(k).wait_recv()
+        total = pair_sum(k, ctx // 2) + row_recv[k].astype(jnp.float32)
+        if k:
+            back_send[k] = total.astype(jnp.bfloat16)
+            give_back(k).start()
+        else:
+            returned[me] = total.astype(jnp.bfloat16)
+
+    for load in loads:
+        load.wait()
+    steps = [0] + order
+    lags = ((forward, 0), (pass_on, 1), (compute, 2), (sum_cores, 3), (sum_rows, 5))
+    for at in range(len(steps) + 5):
+        for stage, lag in lags:
+            if 0 <= at - lag < len(steps):
+                stage(steps[at - lag])
+
+    for k in order:
+        give_back(k).wait_recv()
+    back = returned[...].reshape(combine.shape[1], width)
+    high = combine[...].astype(jnp.bfloat16)
+    low = (combine[...] - high.astype(jnp.float32)).astype(jnp.bfloat16)
+    out_ref[...] = (dot_f32(high, back) + dot_f32(low, back)).astype(jnp.bfloat16)
+    for k in steps:
+        core_swap(k).wait_send()
+        row_swap(k).wait_send()
+        if k:
+            for copy in (dispatch, across, beside, relay, give_back):
+                copy(k).wait_send()
+
+
+def routed_fused(moe_tokens, expert_ids, gate_weights, w_gate, w_up, w_down):
+    token_count, picks = expert_ids.shape
+    model_width = moe_tokens.shape[1]
+    hidden_width = w_gate.shape[2]
+    count = lax.axis_size("exp")
+    width = model_width // lax.axis_size("ctx")
+    capacity = 3 * token_count * picks // (2 * count)
+    targets = slot_targets(expert_ids, count, capacity).reshape(token_count, picks)
+    slots = jnp.arange(count * capacity, dtype=jnp.int32)
+    chosen = jnp.zeros((count * capacity, token_count), jnp.bool_)
+    combine = jnp.zeros((token_count, count * capacity), jnp.float32)
+    for pick in range(picks):
+        chosen = chosen | (slots[:, None] == targets[None, :, pick])
+        combine = combine + jnp.where(
+            slots[None, :] == targets[:, pick : pick + 1], gate_weights[:, pick : pick + 1], 0.0
+        )
+    chosen = chosen.astype(jnp.bfloat16)
+    quarter = lax.dynamic_slice_in_dim(moe_tokens, lax.axis_index("ctx") * width, width, 1)
+    outgoing = jnp.dot(chosen, quarter, preferred_element_type=jnp.float32)
+    outgoing = outgoing.astype(jnp.bfloat16).reshape(count, capacity, width)
+    mine = lax.dynamic_slice_in_dim(chosen, lax.axis_index("exp") * capacity, capacity, 0)
+    own_rows = jnp.dot(mine, moe_tokens, preferred_element_type=jnp.float32).astype(jnp.bfloat16)
+    vmem = pl.BlockSpec(memory_space=pltpu.VMEM)
+    hbm = pl.BlockSpec(memory_space=pl.ANY)
+    block = (capacity, width)
+    dtype = jnp.bfloat16
+    return pl.pallas_call(
+        functools.partial(routed_kernel, count),
+        out_shape=jax.ShapeDtypeStruct((token_count, width), dtype),
+        in_specs=[vmem, vmem, vmem, hbm, hbm, hbm],
+        out_specs=vmem,
+        scratch_shapes=[
+            pltpu.VMEM((model_width, hidden_width), dtype),
+            pltpu.VMEM((model_width, hidden_width), dtype),
+            pltpu.VMEM((hidden_width, model_width), dtype),
+            pltpu.VMEM((4, count) + block, dtype),
+            pltpu.VMEM((count, 2) + block, dtype),
+            pltpu.VMEM((count, 2) + block, dtype),
+            pltpu.VMEM((count, 2) + block, dtype),
+            pltpu.VMEM((count,) + block, dtype),
+            pltpu.VMEM((count,) + block, dtype),
+            pltpu.VMEM((count,) + block, dtype),
+            pltpu.VMEM((count,) + block, dtype),
+            pltpu.SemaphoreType.DMA((3,)),
+            pltpu.SemaphoreType.DMA((1,)),
+        ]
+        + [pltpu.SemaphoreType.DMA((count,))] * 14,
+        compiler_params=pltpu.CompilerParams(
+            collective_id=0, has_side_effects=True, vmem_limit_bytes=56 * 1024 * 1024
+        ),
+    )(outgoing, own_rows, combine, w_gate, w_up, w_down)
+
+
+def shards(
+    queries, latents, block_starts, w_uv, moe_tokens, expert_ids, gate_weights, w_gate, w_up, w_down
+):
+    attended = attention(queries, latents, block_starts, w_uv)
+    count = lax.axis_size("exp")
+    ways = lax.axis_size("ctx")
+    capacity = 3 * expert_ids.shape[0] * expert_ids.shape[1] // (2 * count)
+    fits = ways == 4 and count & (count - 1) == 0 and count >= 4 and capacity % 16 == 0
+    routed = routed_fused if fits and moe_tokens.shape[1] % (128 * ways) == 0 else routed_plain
+    return attended, routed(moe_tokens, expert_ids, gate_weights, w_gate, w_up, w_down)
 
 
 def solution(mesh):

time: 278 us -> 111 us (0.40)
  the two profiles are of different devices: /device:TPU:0 before, /device:TPU:8 now
where the time goes in v1:
time: 111 us; the launch traced here: 110 us
  Pallas kernels  83.2 us (75%)
  blocking collectives  9.17 us (8%)
  local copies, waits for them, and re-layouts  6.66 us (6%)
  matrix products  6.63 us (6%)
  other arithmetic  4 us (4%)
    pallas_call x1, Pallas kernels, routed_fused(): pl.pallas_call(functools.partial(routed_kernel, count), out_shape=jax.Sha...  83.2 us
    all_gather x1, blocking collectives, attention(): shard_piece = lax.all_gather(latents, 'ctx', axis=0, tiled=True)  9.17 us
    unnamed x14, local copies, waits for them, and re-layouts  5.77 us

profile of v1, /device:TPU:8, one launch (start us, length us, event | category | flops | bytes accessed | tf_op | source)
XLA Modules:
  0.0 110.4 jit_solution(3536895064526832788)
XLA Ops:
  0.6 0.0 copy-start
  0.7 0.9 select_reduce_fusion.1
  1.6 0.1 broadcast_in_dim.77
  1.6 0.1 le.16
  1.7 0.7 select_reduce_fusion
  2.5 9.2 %all_gather.3 = bf16[512,576]{0,1:T(8,128)(2,1)} all-gather(bf16[128,576]{0,1:T(8,128)(2,1)} %param.11), channel_id=1, replica_groups=mesh['ctx'=4,'exp'=8] {'ctx'}, dimensions={0}, use_global_device_ids=true | all-gather | bytes 737280 | tf_op jit(solution)/shard_map/all_gather | solution.py:42
  11.7 2.2 %copy.35 = bf16[128,8,576]{2,1,0:T(8,128)(2,1)S(1)} copy(bf16[128,8,576]{0,2,1:T(8,128)(2,1)} %param.10) | data formatting | bytes 2359296 | tf_op args[0]
  13.9 2.1 %fusion = (f32[1024]{0:T(1024)S(1)}, f32[1024,512]{0,1:T(8,128)S(1)}) fusion(s32[1024]{0:T(1024)S(1)} %le.16, s32[512]{0:T(512)S(1)} %fusion.26, bf16[512,576]{0,1:T(8,128)(2,1)} %all_gather.3, bf16[128,8,576]{2,1,0:T(8,128)(2,1)S(1)} %copy.35), kind=kOutput, calls=%fused_computation.5 | convolution fusion | flops 606075904 | bytes 3876864 | tf_op jit(solution)/shard_map/dot_general | solution.py:48
  16.0 0.0 copy-start.1
  16.0 0.6 fusion.4
  16.6 0.4 copy-done.1
  17.1 0.9 fusion.1
  18.0 0.3 copy-done.4
  18.3 0.7 fusion.6
  19.0 0.9 copy.40
  19.9 0.0 copy-done.2
  19.9 0.1 copy.37
  20.0 0.1 eq.122
  20.2 0.7 reduce-window.6
  20.9 0.2 slice_reduce_fusion
  21.2 0.1 eq.118
  21.3 0.1 fusion.20
  21.4 0.1 reduce_sum.42
  21.6 0.1 copy.39
  21.6 0.0 copy-done
  21.7 0.0 copy-start.3
  21.7 1.6 %convolution_convert_fusion.1 = bf16[384,1792]{1,0:T(8,128)(2,1)} fusion(bf16[128,7168]{1,0:T(8,128)(2,1)S(1)} %copy-done, s32[]{:T(128)S(6)} %select_n.71, s32[128]{0:T(128)S(1)} %get-tuple-element.15, s32[128]{0:T(128)S(1)} %get-tuple-element.14), kind=kOutput, calls=%fused_computation.1 | convolution fusion | flops 176996352 | bytes 1836036 | tf_op jit(solution)/shard_map/dot_general | solution.py:313
  23.3 1.3 %convolution_convert_fusion.own_rows = bf16[48,7168]{1,0:T(8,128)(2,1)} fusion(bf16[128,7168]{1,0:T(8,128)(2,1)S(1)} %copy-done, pred[384,128]{1,0:T(8,128)(4,1)S(1)} %fusion.17, s32[]{:T(128)S(6)} %select_n.72), kind=kOutput, calls=%fused_computation | convolution fusion | flops 88424448 | bytes 2529284 | tf_op jit(solution)/shard_map/dot_general | solution.py:316
  24.6 0.0 copy-done.3
  24.6 0.8 select_add_fusion.combine
  25.4 83.2 %shard_map.113 = bf16[128,1792]{1,0:T(8,128)(2,1)} custom-call(bf16[8,48,1792]{2,1,0:T(8,128)(2,1)} %bitcast.29, bf16[48,7168]{1,0:T(8,128)(2,1)} %convolution_convert_fusion.own_rows, f32[128,384]{1,0:T(8,128)} %select_add_fusion.combine, bf16[1,7168,128]{2,1,0:T(8,128)(2,1)} %gate_hbm.1, bf16[1,7168,128]{2,1,0:T(8,128)(2,1)} %up_hbm.1, ...), custom_call_target="tpu_custom_call" | custom-call | tf_op jit(solution)/shard_map/pallas_call | solution.py:321
  108.6 1.8 %copy.44 = bf16[128,1792]{1,0:T(8,128)(2,1)} copy(bf16[128,1792]{1,0:T(8,128)(2,1)} %shard_map.113) | data formatting | bytes 917504
  (14 shorter events, 0.2 us)
Async XLA Ops:
  0.6 21.0 %copy-start = (bf16[128,7168]{1,0:T(8,128)(2,1)S(1)}, bf16[128,7168]{1,0:T(8,128)(2,1)}, u32[]{:S(2)}) copy-start(bf16[128,7168]{1,0:T(8,128)(2,1)} %param.14) | copy-start | bytes 5505028
  16.0 1.1 copy-start.1
  17.0 1.2 %copy-start.4 = (bf16[8,512,128]{2,1,0:T(8,128)(2,1)S(1)}, bf16[8,512,128]{2,1,0:T(8,128)(2,1)}, u32[]{:S(2)}) copy-start(bf16[8,512,128]{2,1,0:T(8,128)(2,1)} %param.13) | copy-start | bytes 3145732
  18.3 1.6 %copy-start.2 = (s32[128,2]{0,1:T(2,128)S(1)}, s32[128,2]{0,1:T(2,128)}, u32[]{:S(2)}) copy-start(s32[128,2]{0,1:T(2,128)} %param.15) | copy-start | bytes 3076
  21.7 2.9 %copy-start.3 = (f32[128,2]{0,1:T(2,128)S(1)}, f32[128,2]{0,1:T(2,128)}, u32[]{:S(2)}) copy-start(f32[128,2]{0,1:T(2,128)} %param.16) | copy-start | bytes 3076

commit v2 on v1

--- a/solution.py
+++ b/solution.py
@@ -116,15 +116,41 @@
     return flipped
 
 
-def step_order(count):
+def plan(count, heads):
     half = count // 2
     near, far = list(range(1, half)), list(range(half, count))
-    order = []
-    for at in range(half):
+    left = list(range(heads))
+    order = [("forward", near[0]), ("compute", 0)]
+    order += [("forward", k) for k in near[1:]]
+    order += [("pass_on", near[0]), ("sum_cores", 0), ("latents", 0)]
+    for at, k in enumerate(near):
+        order += [("attend", left.pop(0)) for _ in range(min(1, len(left)))]
+        if at + 1 < len(near):
+            order += [("pass_on", near[at + 1])]
+        order += [("compute", k)]
+        if at:
+            order += [("sum_cores", near[at - 1])]
+        else:
+            order += [("sum_rows", 0)]
+    order += [("forward", far[0]), ("sum_cores", near[-1])]
+    for at, k in enumerate(far):
+        if at:
+            order += [("forward", k), ("sum_cores", far[at - 1])]
         if at < len(near):
-            order.append(near[at])
-        order.append(far[at])
-    return order
+            order += [("sum_rows", near[at])]
+        share = -(-len(left) // max(1, len(far) - 1 - at))
+        order += [("attend", left.pop(0)) for _ in range(min(share, len(left)))]
+        order += [("pass_on", k)]
+        if at:
+            order += [("sum_rows", far[at - 1])]
+        order += [("compute", k)]
+    return order + [("sum_cores", far[-1]), ("sum_rows", far[-1])]
+
+
+def dot_first(left, right):
+    return lax.dot_general(
+        left, right, (((0,), (0,)), ((), ())), preferred_element_type=jnp.float32
+    )
 
 
 def dot_f32(left, right):
@@ -132,9 +158,10 @@
 
 
 def routed_kernel(
-    count, outgoing, own_rows, combine, gate_hbm, up_hbm, down_hbm, out_ref,
-    gate_w, up_w, down_w, arrived, kept, core_send, core_recv, row_send, row_recv,
-    back_send, returned, load_sem, own_sem,
+    count, outgoing, own_rows, combine, latents, starts, gate_hbm, up_hbm, down_hbm,
+    queries_hbm, uv_hbm, out_ref, attended_ref,
+    gate_w, up_w, down_w, query_t, uv_w, every_latent, value_t, seen, arrived, kept, core_send, core_recv, row_send, row_recv,
+    back_send, returned, load_sem, lat_s, lat_r,
     out_s, out_r, side_s, side_r, near_s, near_r, relay_s, relay_r,
     core_s, core_r, row_s, row_r, back_s, back_r,
 ):
@@ -149,6 +176,8 @@
         pltpu.make_async_copy(gate_hbm.at[0], gate_w, load_sem.at[0]),
         pltpu.make_async_copy(up_hbm.at[0], up_w, load_sem.at[1]),
         pltpu.make_async_copy(down_hbm.at[0], down_w, load_sem.at[2]),
+        pltpu.make_async_copy(queries_hbm, query_t, load_sem.at[3]),
+        pltpu.make_async_copy(uv_hbm, uv_w, load_sem.at[4]),
     ]
     for load in loads:
         load.start()
@@ -206,9 +235,54 @@
             back_send.at[k], returned.at[me], back_s.at[k], back_r.at[k], to, ctx
         )
 
-    order = step_order(count)
-    for k in order:
+    def own_latents(step, peer):
+        return remote(
+            latents, every_latent.at[ctx], lat_s.at[step], lat_r.at[step], me, peer
+        )
+
+    row_block = every_latent.at[other_row]
+    latents_beside = own_latents(0, other_core)
+    latents_across = own_latents(1, other_row)
+    latents_relay = remote(row_block, row_block, lat_s.at[2], lat_r.at[2], me, other_core)
+    latents_across.start()
+    latents_beside.start()
+    partners = list(range(1, count))
+    for k in partners:
         dispatch(k).start()
+    every_latent[ctx] = latents[...]
+
+    tokens = latents.shape[0]
+    half_block = tokens // 2
+    lat_width = uv_w.shape[1]
+
+    def gather_latents(_):
+        latents_across.wait_recv()
+        latents_relay.start()
+        key_at = lax.broadcasted_iota(jnp.int32, (4 * tokens, tokens), 0)
+        own_at = lax.broadcasted_iota(jnp.int32, (4 * tokens, tokens), 1)
+        key_block = key_at // half_block
+        key_start = jnp.zeros_like(key_at)
+        for block in range(8):
+            key_start = jnp.where(key_block == block, starts[block], key_start)
+        own_start = jnp.where(own_at < half_block, starts[2 * ctx], starts[2 * ctx + 1])
+        key_position = key_start + key_at % half_block
+        seen[...] = (key_position <= own_start + own_at % half_block).astype(jnp.float32)
+        latents_beside.wait_recv()
+        latents_relay.wait_recv()
+        for block in range(4):
+            value_t[:, pl.ds(block * tokens, tokens)] = every_latent[block, :, :lat_width].T
+
+    def attend(head):
+        keys = every_latent[...].reshape(4 * tokens, latents.shape[1])
+        scores = dot_f32(keys, query_t[head]) * score_scale
+        visible = seen[...] > 0.5
+        masked = jnp.where(visible, scores, neg_fill)
+        top = jnp.max(masked, axis=0, keepdims=True)
+        weights = jnp.where(visible, jnp.exp(masked - top), 0.0)
+        totals = jnp.sum(weights, axis=0, keepdims=True)
+        blended = dot_f32(value_t[...], weights.astype(jnp.bfloat16))
+        latent_out = (blended / totals).astype(jnp.bfloat16)
+        attended_ref[head] = dot_first(latent_out, uv_w[head]).astype(jnp.bfloat16)
 
     def columns(at):
         return pl.ds(pl.multiple_of(at * width, 128), width)
@@ -269,22 +343,26 @@
         else:
             returned[me] = total.astype(jnp.bfloat16)
 
-    for load in loads:
-        load.wait()
-    steps = [0] + order
-    lags = ((forward, 0), (pass_on, 1), (compute, 2), (sum_cores, 3), (sum_rows, 5))
-    for at in range(len(steps) + 5):
-        for stage, lag in lags:
-            if 0 <= at - lag < len(steps):
-                stage(steps[at - lag])
-
-    for k in order:
+    stages = {
+        "forward": forward, "pass_on": pass_on, "compute": compute, "sum_cores": sum_cores,
+        "sum_rows": sum_rows, "attend": attend, "latents": gather_latents,
+    }
+    waiting = list(loads)
+    for stage, at in plan(count, query_t.shape[0]):
+        if stage == "compute":
+            while waiting:
+                waiting.pop(0).wait()
+        stages[stage](at)
+
+    for k in partners:
         give_back(k).wait_recv()
     back = returned[...].reshape(combine.shape[1], width)
     high = combine[...].astype(jnp.bfloat16)
     low = (combine[...] - high.astype(jnp.float32)).astype(jnp.bfloat16)
     out_ref[...] = (dot_f32(high, back) + dot_f32(low, back)).astype(jnp.bfloat16)
-    for k in steps:
+    for copy in (latents_across, latents_beside, latents_relay):
+        copy.wait_send()
+    for k in [0] + partners:
         core_swap(k).wait_send()
         row_swap(k).wait_send()
         if k:
@@ -292,7 +370,13 @@
                 copy(k).wait_send()
 
 
-def routed_fused(moe_tokens, expert_ids, gate_weights, w_gate, w_up, w_down):
+def window_fused(
+    queries, latents, block_starts, w_uv, moe_tokens, expert_ids, gate_weights, w_gate, w_up, w_down
+):
+    queries = jnp.transpose(queries, (1, 2, 0))
+    heads, entry_width, query_tokens = queries.shape
+    lat_width, value_width = w_uv.shape[1:]
+    key_count = lax.axis_size("ctx") * query_tokens
     token_count, picks = expert_ids.shape
     model_width = moe_tokens.shape[1]
     hidden_width = w_gate.shape[2]
@@ -318,15 +402,23 @@
     hbm = pl.BlockSpec(memory_space=pl.ANY)
     block = (capacity, width)
     dtype = jnp.bfloat16
-    return pl.pallas_call(
+    routed, attended = pl.pallas_call(
         functools.partial(routed_kernel, count),
-        out_shape=jax.ShapeDtypeStruct((token_count, width), dtype),
-        in_specs=[vmem, vmem, vmem, hbm, hbm, hbm],
-        out_specs=vmem,
+        out_shape=(
+            jax.ShapeDtypeStruct((token_count, width), dtype),
+            jax.ShapeDtypeStruct((heads, query_tokens, value_width), dtype),
+        ),
+        in_specs=[vmem] * 4 + [pl.BlockSpec(memory_space=pltpu.SMEM)] + [hbm] * 5,
+        out_specs=(vmem, vmem),
         scratch_shapes=[
             pltpu.VMEM((model_width, hidden_width), dtype),
             pltpu.VMEM((model_width, hidden_width), dtype),
             pltpu.VMEM((hidden_width, model_width), dtype),
+            pltpu.VMEM(queries.shape, dtype),
+            pltpu.VMEM(w_uv.shape, dtype),
+            pltpu.VMEM((4,) + latents.shape, dtype),
+            pltpu.VMEM((lat_width, key_count), dtype),
+            pltpu.VMEM((key_count, query_tokens), jnp.float32),
             pltpu.VMEM((4, count) + block, dtype),
             pltpu.VMEM((count, 2) + block, dtype),
             pltpu.VMEM((count, 2) + block, dtype),
@@ -335,26 +427,36 @@
             pltpu.VMEM((count,) + block, dtype),
             pltpu.VMEM((count,) + block, dtype),
             pltpu.VMEM((count,) + block, dtype),
+            pltpu.SemaphoreType.DMA((5,)),
             pltpu.SemaphoreType.DMA((3,)),
-            pltpu.SemaphoreType.DMA((1,)),
+            pltpu.SemaphoreType.DMA((3,)),
         ]
         + [pltpu.SemaphoreType.DMA((count,))] * 14,
         compiler_params=pltpu.CompilerParams(
             collective_id=0, has_side_effects=True, vmem_limit_bytes=56 * 1024 * 1024
         ),
-    )(outgoing, own_rows, combine, w_gate, w_up, w_down)
+    )(
+        outgoing, own_rows, combine, latents, block_starts, w_gate, w_up, w_down, queries, w_uv
+    )
+    return jnp.transpose(attended, (1, 0, 2)), routed
 
 
 def shards(
     queries, latents, block_starts, w_uv, moe_tokens, expert_ids, gate_weights, w_gate, w_up, w_down
 ):
-    attended = attention(queries, latents, block_starts, w_uv)
     count = lax.axis_size("exp")
     ways = lax.axis_size("ctx")
-    capacity = 3 * expert_ids.shape[0] * expert_ids.shape[1] // (2 * count)
+    token_count, picks = expert_ids.shape
+    capacity = 3 * token_count * picks // (2 * count)
     fits = ways == 4 and count & (count - 1) == 0 and count >= 4 and capacity % 16 == 0
-    routed = routed_fused if fits and moe_tokens.shape[1] % (128 * ways) == 0 else routed_plain
-    return attended, routed(moe_tokens, expert_ids, gate_weights, w_gate, w_up, w_down)
+    fits = fits and moe_tokens.shape[1] % (128 * ways) == 0 and block_starts.shape[0] == 8
+    if fits:
+        return window_fused(
+            queries, latents, block_starts, w_uv, moe_tokens, expert_ids, gate_weights,
+            w_gate, w_up, w_down,
+        )
+    attended = attention(queries, latents, block_starts, w_uv)
+    return attended, routed_plain(moe_tokens, expert_ids, gate_weights, w_gate, w_up, w_down)
 
 
 def solution(mesh):

time: 111 us -> 111 us (level)
  the two profiles are of different devices: /device:TPU:8 before, /device:TPU:0 now
where the time goes in v2:
time: 111 us
  Pallas kernels  97.2 us (88%)
  local copies, waits for them, and re-layouts  7.68 us (7%)
  matrix products  2.87 us (3%)
  other arithmetic  2.28 us (2%)
    pallas_call x1, Pallas kernels, window_fused(): pl.pallas_call(functools.partial(routed_kernel, count), out_shape=(jax.Sh...  97.2 us
    unnamed x6, local copies, waits for them, and re-layouts  6.15 us

profile of v2, /device:TPU:0, one launch (start us, length us, event | category | flops | bytes accessed | tf_op | source)
XLA Modules:
  0.0 110.7 jit_solution(386240892140225123)
XLA Ops:
  0.6 0.0 copy-start
  0.7 0.8 slice_bitcast_fusion.1
  1.5 0.8 copy.26
  2.3 0.1 eq.86
  2.4 0.1 eq.82
  2.6 0.6 reduce-window.6
  3.1 0.2 slice_reduce_fusion
  3.4 0.1 fusion.4
  3.5 0.1 reduce_sum.12
  3.6 0.1 copy.28
  3.7 0.7 multiply_add_fusion
  4.5 1.7 %copy.29.latents = bf16[128,576]{1,0:T(8,128)(2,1)} copy(bf16[128,576]{0,1:T(8,128)(2,1)} %param.11) | data formatting | bytes 294912 | tf_op args[1]
  6.2 0.8 select_add_fusion.combine
  7.0 0.0 copy-done
  7.0 1.3 %convolution_convert_fusion.own_rows = bf16[48,7168]{1,0:T(8,128)(2,1)} fusion(bf16[128,7168]{1,0:T(8,128)(2,1)S(1)} %copy-done, pred[384,128]{1,0:T(8,128)(4,1)S(1)} %fusion.1, s32[]{:T(128)S(6)} %select_n.14), kind=kOutput, calls=%fused_computation | convolution fusion | flops 88424448 | bytes 2529284 | tf_op jit(solution)/shard_map/dot_general | solution.py:400
  8.3 1.6 %convolution_convert_fusion.1 = bf16[384,1792]{1,0:T(8,128)(2,1)} fusion(bf16[128,7168]{1,0:T(8,128)(2,1)S(1)} %copy-done, s32[]{:T(128)S(6)} %select_n.13, s32[128]{0:T(128)S(1)} %get-tuple-element.17, s32[128]{0:T(128)S(1)} %get-tuple-element.16), kind=kOutput, calls=%fused_computation.1 | convolution fusion | flops 176996352 | bytes 1836036 | tf_op jit(solution)/shard_map/dot_general | solution.py:397
  9.9 97.2 %shard_map.113 = (bf16[128,1792]{1,0:T(8,128)(2,1)}, bf16[8,128,128]{2,1,0:T(8,128)(2,1)}) custom-call(bf16[8,48,1792]{2,1,0:T(8,128)(2,1)} %bitcast.20, bf16[48,7168]{1,0:T(8,128)(2,1)} %convolution_convert_fusion.own_rows, f32[128,384]{1,0:T(8,128)} %select_add_fusion.combine, bf16[128,576]{1,0:T(8,128)(2,1)} %copy.29.latents, s32[8]{0:T(128)} %starts.1, ...), custom_call_target="tpu_custom_call" | custom-call | tf_op jit(solution)/shard_map/pallas_call | solution.py:405
  107.1 1.8 %copy.30 = bf16[128,8,128]{2,1,0:T(8,128)(2,1)} copy(bf16[128,8,128]{2,0,1:T(8,128)(2,1)} %bitcast.22) | data formatting | bytes 524288
  108.9 1.8 %copy.32 = bf16[128,1792]{1,0:T(8,128)(2,1)} copy(bf16[128,1792]{1,0:T(8,128)(2,1)} %get-tuple-element.21) | data formatting | bytes 917504
  (5 shorter events, 0.1 us)
Async XLA Ops:
  0.6 6.4 %copy-start = (bf16[128,7168]{1,0:T(8,128)(2,1)S(1)}, bf16[128,7168]{1,0:T(8,128)(2,1)}, u32[]{:S(2)}) copy-start(bf16[128,7168]{1,0:T(8,128)(2,1)} %param.14) | copy-start | bytes 5505028
